TPU v7x, 32 devices: a whole 2x2x4 slice. The times are simulated.
32 devices in a mesh: grp: 2 (over x), seq: 16 (over z, y, core).
Axes of the slice: x: 2, y: 2, z: 4, core: 2. Of those that a mesh axis runs over, the one named last changes fastest.
Arguments:
- queries: bfloat16 [8, 4096], P('grp', 'seq'), parts along dimension 0, may hold values from -40 to 40
- gate_logits: float32 [8, 64], P('grp'), parts along dimension 0, may hold values from -6 to 6
- kv_pool: bfloat16 [512, 128, 2048], P(('grp', 'seq')), parts along dimension 0, may hold values from -6 to 6
- page_table: int32 [8, 64], P('grp'), parts along dimension 0, may hold values from 0 to 255, as said below
- selected: int32 [8, 8, 16], P('grp'), parts along dimension 0, may hold values from 0 to 63, as said below
- lengths: int32 [8], P('grp'), parts along dimension 0, may hold values from 4096 to 8192, as said below
Outputs:
- attended: bfloat16 [8, 4096], P('grp', 'seq'), parts along dimension 0
There are 2 independent parts, one for each index of `grp`. A program takes and returns all parts, laid end to end along the dimension named above; each array names one. Nothing has to cross between parts.
Inputs may be any that keep to these rules, and one draw needn't show every extreme that they name: `page_table`: a one-to-one map of the 4 x 64 pages onto the pool slots; each aligned run of 2 pages of a request lies in 2 consecutive slots starting at a multiple of 2. `lengths`: some request in every draw has length 8192. `selected`: for each request and key-value head, 16 different pages, all among the request's last 32 live pages, the last live page among them.
All inputs are finite; a program needn't handle non-finite values.
Results may differ from a plain program's by a relative error of at most 0.0039.
Values may be sent and summed in bfloat16 or wider, within the bound.
A program may use at most 64 MiB of HBM per device.

v0:
```python
import math
import jax
import jax.numpy as jnp
from jax import lax
from jax.sharding import PartitionSpec as P

HEAD_DIM = 128
neg_big = -1e30


def joined(part, axis, combine):
    gathered = jax.tree.map(lambda a: lax.all_gather(a, axis), part)

    def take(source):
        return jax.tree.map(lambda a: lax.dynamic_index_in_dim(a, source, 0, False), gathered)

    return lax.fori_loop(
        1, lax.axis_size(axis), lambda source, state: combine(state, take(source)), take(0)
    )


def merge_pair(left, right):
    merged = ()
    for offset in (0, 3):
        row_top = jnp.maximum(left[offset], right[offset])
        left_scale = jnp.exp(left[offset] - row_top)
        right_scale = jnp.exp(right[offset] - row_top)
        merged = merged + (
            row_top,
            left[offset + 1] * left_scale + right[offset + 1] * right_scale,
            left[offset + 2] * left_scale[..., None] + right[offset + 2] * right_scale[..., None],
        )
    return merged


def per_device(queries, gate_logits, kv_pool, page_table, selected, lengths):
    slot_count, page_len, double_width = kv_pool.shape
    kv_width = double_width // 2
    kv_heads = kv_width // HEAD_DIM
    requests = page_table.shape[0]
    ctx_pages = page_table.shape[1]
    col_count = queries.shape[1]
    highest = lax.Precision.HIGHEST
    all_queries = lax.all_gather(queries, "seq", axis=1, tiled=True)
    head_count = all_queries.shape[1] // HEAD_DIM
    group_size = head_count // kv_heads
    score_scale = 1.0 / math.sqrt(HEAD_DIM)
    first_slot = lax.axis_index("seq") * slot_count
    slot_ids = first_slot + jnp.arange(slot_count, dtype=jnp.int32)
    slot_match = page_table[:, :, None] == slot_ids[None, None, :]
    owner_hot = jnp.any(slot_match, axis=1)
    page_index = jnp.arange(ctx_pages, dtype=jnp.int32)
    page_of = jnp.sum(jnp.where(slot_match, page_index[None, :, None], 0), axis=(0, 1))
    slot_len = jnp.sum(jnp.where(owner_hot, lengths[:, None], 0), axis=0)
    owner_rows = jnp.dot(
        owner_hot.T.astype(jnp.bfloat16), all_queries, preferred_element_type=jnp.float32
    ).astype(jnp.bfloat16)
    slot_queries = owner_rows.reshape(slot_count, kv_heads, group_size, HEAD_DIM)
    key_rows = kv_pool[:, :, :kv_width].reshape(slot_count, page_len, kv_heads, HEAD_DIM)
    value_rows = kv_pool[:, :, kv_width:].reshape(slot_count, page_len, kv_heads, HEAD_DIM)
    position = page_of[:, None] * page_len + jnp.arange(page_len, dtype=jnp.int32)[None, :]
    is_valid = position < slot_len[:, None]
    is_live = page_of * page_len < slot_len
    valid_bf = is_valid.astype(jnp.bfloat16)
    counts = jnp.maximum(jnp.sum(is_valid.astype(jnp.float32), axis=1), 1.0)
    summary_keys = (
        jnp.einsum("st,stkd->skd", valid_bf, key_rows, preferred_element_type=jnp.float32)
        / counts[:, None, None]
    ).astype(jnp.bfloat16)
    summary_values = (
        jnp.einsum("st,stkd->skd", valid_bf, value_rows, preferred_element_type=jnp.float32)
        / counts[:, None, None]
    ).astype(jnp.bfloat16)
    coarse = (
        jnp.einsum("skgd,skd->skg", slot_queries, summary_keys, preferred_element_type=jnp.float32)
        * score_scale
    )
    coarse_mask = owner_hot[:, :, None, None] & is_live[None, :, None, None]
    coarse_masked = jnp.where(coarse_mask, coarse[None], neg_big)
    coarse_top = jnp.max(coarse_masked, axis=1)
    coarse_wt = jnp.where(coarse_mask, jnp.exp(coarse_masked - coarse_top[:, None]), 0.0)
    coarse_sum = jnp.sum(coarse_wt, axis=1)
    coarse_num = jnp.einsum(
        "rskg,skd->rkgd", coarse_wt, summary_values.astype(jnp.float32), precision=highest
    )
    fine_scores = (
        jnp.einsum("skgd,stkd->skgt", slot_queries, key_rows, preferred_element_type=jnp.float32)
        * score_scale
    )
    token_mask = is_valid[:, None, None, :]
    fine_masked = jnp.where(token_mask, fine_scores, neg_big)
    page_max = jnp.max(fine_masked, axis=3)
    page_wt = jnp.where(token_mask, jnp.exp(fine_masked - page_max[..., None]), 0.0).astype(
        jnp.bfloat16
    )
    page_sum = jnp.sum(page_wt.astype(jnp.float32), axis=3)
    page_num = jnp.einsum(
        "skgt,stkd->skgd", page_wt, value_rows, preferred_element_type=jnp.float32
    )
    page_hit = selected[:, None, :, :] == page_of[None, :, None, None]
    chosen = jnp.any(page_hit, axis=3) & owner_hot[:, :, None]
    chosen_full = chosen[..., None]
    sel_masked = jnp.where(chosen_full, page_max[None], neg_big)
    fine_top = jnp.max(sel_masked, axis=1)
    fine_wt = jnp.where(chosen_full, jnp.exp(sel_masked - fine_top[:, None]), 0.0)
    fine_sum = jnp.sum(fine_wt * page_sum[None], axis=1)
    fine_num = jnp.einsum("rskg,skgd->rkgd", fine_wt, page_num, precision=highest)
    gate_all = jax.nn.sigmoid(gate_logits)
    start_col = lax.axis_index("seq") * col_count
    coarse_gate = lax.dynamic_slice_in_dim(
        jnp.repeat(gate_all[:, :head_count], HEAD_DIM, axis=1), start_col, col_count, 1
    )
    fine_gate = lax.dynamic_slice_in_dim(
        jnp.repeat(gate_all[:, head_count:], HEAD_DIM, axis=1), start_col, col_count, 1
    )
    merged = joined(
        (coarse_top, coarse_sum, coarse_num, fine_top, fine_sum, fine_num), "seq", merge_pair
    )
    coarse_full = (merged[2] / merged[1][..., None]).reshape(requests, head_count * HEAD_DIM)
    fine_full = (merged[5] / merged[4][..., None]).reshape(requests, head_count * HEAD_DIM)
    coarse_cols = lax.dynamic_slice_in_dim(coarse_full, start_col, col_count, 1)
    fine_cols = lax.dynamic_slice_in_dim(fine_full, start_col, col_count, 1)
    return (coarse_gate * coarse_cols + fine_gate * fine_cols).astype(jnp.bfloat16)


def solution(mesh):
    return jax.shard_map(
        per_device,
        mesh=mesh,
        in_specs=(
            P("grp", "seq"),
            P("grp", None),
            P(("grp", "seq"), None, None),
            P("grp", None),
            P("grp", None, None),
            P("grp"),
        ),
        out_specs=P("grp", "seq"),
        check_vma=False,
    )
```

profile of v0, /device:TPU:0, one launch (start us, length us, event | category | flops | bytes accessed | tf_op | source)
XLA Modules:
  0.0 191.3 jit_solution(17139264196177832659)
XLA Ops:
  9.3 23.4 %all_gather.39 = bf16[4,4096]{1,0:T(4,128)(2,1)S(1)} all-gather(bf16[4,256]{1,0:T(4,128)(2,1)} %param.8), channel_id=1, replica_groups=mesh['grp'=2,'seq'=16] {'seq'}, dimensions={1}, use_global_device_ids=true | all-gather | bytes 34816 | tf_op jit(solution)/shard_map/all_gather | solution.py:44
  33.1 6.1 %fusion.43 = (bf16[16,128,1024]{2,1,0:T(8,128)(2,1)}, bf16[16,128,1024]{2,1,0:T(8,128)(2,1)}) fusion(bf16[16,128,2048]{2,1,0:T(8,128)(2,1)} %param.10), kind=kLoop, calls=%fused_computation.82 | loop fusion | bytes 16777216 | tf_op jit(solution)/shard_map/slice | solution.py:60
  39.2 6.4 %copy.115 = bf16[16,128,1024]{1,2,0:T(8,128)(2,1)} copy(bf16[16,128,1024]{2,1,0:T(8,128)(2,1)} %get-tuple-element.421) | data formatting | bytes 8388608
  45.6 6.4 %copy.114 = bf16[16,128,1024]{1,2,0:T(8,128)(2,1)} copy(bf16[16,128,1024]{2,1,0:T(8,128)(2,1)} %get-tuple-element.422) | data formatting | bytes 8388608
  52.0 3.5 %fusion.31 = f32[16,1,8,128]{3,1,2,0:T(1,128)S(1)} fusion(bf16[16,128,8,128]{1,3,2,0:T(8,128)(2,1)} %bitcast.92, pred[16,128,1,1]{1,0,2,3:T(8,128)(4,1)S(1)} %get-tuple-element.428), kind=kOutput, calls=%fused_computation.61 | convolution fusion | flops 4194304 | bytes 4261888 | tf_op jit(solution)/shard_map/st,stkd->skd/dot_general | solution.py:71
  55.5 1.2 fusion.33
  58.5 1.2 compare_reduce_fusion
  59.9 3.5 %fusion.45 = (f32[16,8,4]{2,1,0:T(8,128)S(1)}, f32[16,8,4,128]{3,2,1,0:T(4,128)S(1)}) fusion(bf16[16,8,4,128]{3,2,1,0:T(4,128)(2,1)S(1)} %reshape.105, bf16[16,128,8,128]{1,3,2,0:T(8,128)(2,1)} %bitcast.94, pred[16,128]{1,0:T(8,128)(4,1)S(1)} %get-tuple-element.427), kind=kOutput, calls=%fused_computation.84 | convolution fusion | flops 16973312 | bytes 4591616 | tf_op jit(solution)/shard_map/skgd,stkd->skgt/dot_general | solution.py:87
  63.7 4.5 %fusion.40 = f32[16,8,4,128]{3,2,1,0:T(4,128)S(1)} fusion(bf16[16,128,8,128]{1,3,2,0:T(8,128)(2,1)} %bitcast.93, f32[16,8,4,128]{3,2,1,0:T(4,128)S(1)} %get-tuple-element.430, f32[16,8,4]{2,1,0:T(8,128)S(1)} %get-tuple-element.429, pred[16,128]{1,0:T(8,128)(4,1)S(1)} %get-tuple-element.427), kind=kOutput, calls=%fused_computation.81 | convolution fusion | flops 16973824 | bytes 4722688 | tf_op jit(solution)/shard_map/skgt,stkd->skgd/dot_general | solution.py:97
  70.9 18.0 %all-gather.1 = f32[64,8,4]{1,2,0:T(4,128)S(1)} all-gather(f32[4,8,4]{1,2,0:T(4,128)S(1)} %copy.87), channel_id=3, replica_groups=mesh['grp'=2,'seq'=16] {'seq'}, dimensions={0}, use_global_device_ids=true | all-gather | bytes 8704 | tf_op jit(solution)/shard_map/all_gather | solution.py:12
  88.9 19.0 %all-gather = f32[64,8,4]{1,2,0:T(4,128)S(1)} all-gather(f32[4,8,4]{1,2,0:T(4,128)S(1)} %copy.86), channel_id=2, replica_groups=mesh['grp'=2,'seq'=16] {'seq'}, dimensions={0}, use_global_device_ids=true | all-gather | bytes 8704 | tf_op jit(solution)/shard_map/all_gather | solution.py:12
  107.9 18.0 %all-gather.4 = f32[64,8,4]{1,2,0:T(4,128)S(1)} all-gather(f32[4,8,4]{1,2,0:T(4,128)S(1)} %copy.95), channel_id=6, replica_groups=mesh['grp'=2,'seq'=16] {'seq'}, dimensions={0}, use_global_device_ids=true | all-gather | bytes 8704 | tf_op jit(solution)/shard_map/all_gather | solution.py:12
  125.9 19.0 %all-gather.3 = f32[64,8,4]{1,2,0:T(4,128)S(1)} all-gather(f32[4,8,4]{1,2,0:T(4,128)S(1)} %copy.93), channel_id=5, replica_groups=mesh['grp'=2,'seq'=16] {'seq'}, dimensions={0}, use_global_device_ids=true | all-gather | bytes 8704 | tf_op jit(solution)/shard_map/all_gather | solution.py:12
  146.7 36.7 %while.25 = (s32[]{:T(128)}, f32[4,8,4]{1,2,0:T(4,128)S(1)}, f32[4,8,4]{1,2,0:T(4,128)S(1)}, f32[4,8,4,128]{3,2,1,0:T(4,128)S(1)}, f32[4,8,4]{1,2,0:T(4,128)S(1)...) while((s32[]{:T(128)}, f32[4,8,4]{1,2,0:T(4,128)S(1)}, ...), condition=%wide.region_12.13_spmd, body=%wide.region_11.12_spmd.sunk | while | flops 99845 | bytes 538823 | solution.py:17
  148.0 1.1 fusion.60
  150.4 1.1 fusion.60
  152.9 1.1 fusion.60
  155.3 1.1 fusion.60
  157.8 1.1 fusion.60
  160.2 1.1 fusion.60
  162.7 1.1 fusion.60
  170.0 1.1 fusion.60
  174.9 1.1 fusion.60
  179.8 1.1 fusion.60
  (174 shorter events, 35.8 us)
Async XLA Ops:
  6.5 138.4 %all-gather.9.cloned.1.call-start = ((), (), s32[]{:S(2)}) async-start(), calls=%async_computation | async-start | bytes 1114112 | tf_op jit(solution)/shard_map/all_gather | solution.py:12
  52.0 3.5 %copy-start = (bf16[16,128,1024]{1,2,0:T(8,128)(2,1)S(1)}, bf16[16,128,1024]{1,2,0:T(8,128)(2,1)}, u32[]{:S(2)}) copy-start(bf16[16,128,1024]{1,2,0:T(8,128)(2,1)} %copy.114) | copy-start | bytes 12582916
  52.0 6.5 %copy-start.1 = (s32[4,8,16]{2,1,0:T(8,128)S(1)}, s32[4,8,16]{2,1,0:T(8,128)}, u32[]{:S(2)}) copy-start(s32[4,8,16]{2,1,0:T(8,128)} %param.12) | copy-start | bytes 6148
  58.5 87.3 %all-gather.11.cloned.1.call-start = ((), (), s32[]{:S(2)}) async-start(), calls=%async_computation.1 | async-start | bytes 1114112 | tf_op jit(solution)/shard_map/all_gather | solution.py:12
  59.9 9.7 %copy-start.2 = (f32[4,64]{1,0:T(4,128)S(1)}, f32[4,64]{1,0:T(4,128)}, u32[]{:S(2)}) copy-start(f32[4,64]{1,0:T(4,128)} %param.9) | copy-start | bytes 3076
Sparse Core Ops, SparseCore 0:
  58.6 34.1 all-gather.8
  94.9 37.5 all-gather.10
where the time goes:
time: 193 us; the launch traced here: 191 us
  blocking collectives  97.4 us (50%)
  local copies, waits for them, and re-layouts  41.4 us (21%)
  other arithmetic  23.8 us (12%)
  matrix products  14.6 us (8%)
  between operations  13.6 us (7%)
    all_gather x4, blocking collectives, joined(): gathered = jax.tree.map(lambda a: lax.all_gather(a, axis), part)  74 us
    all_gather x1, blocking collectives, per_device(): all_queries = lax.all_gather(queries, 'seq', axis=1, tiled=True)  23.4 us
    add x15, other arithmetic, merge_pair(): left[offset + 2] * left_scale[..., None]  16.9 us
    dynamic_slice x21, local copies, waits for them, and re-layouts, take(): lax.dynamic_index_in_dim(a, source, 0, False)  14.4 us
    unnamed x11, local copies, waits for them, and re-layouts  13 us
    slice x1, local copies, waits for them, and re-layouts, per_device(): kv_pool[:, :, kv_width:].reshape(slot_count, page_len, kv_heads, HEAD_DIM)  6.11 us
    dot_general x1, matrix products, per_device(): jnp.einsum('skgt,stkd->skgd', page_wt, value_rows, preferred_element_type...  4.5 us
  transfers between devices with their start and end apart: 2, of which 0 were waited for; matrix products, arithmetic and copies ran while one was open for 7% of the time, Pallas kernels for 0%

commit v1 on v0

--- a/solution.py
+++ b/solution.py
@@ -6,6 +6,11 @@
 
 HEAD_DIM = 128
 neg_big = -1e30
+
+
+def gather_blocks(block, mesh_axis, dim):
+    blocks = lax.all_gather(block, mesh_axis)
+    return jnp.concatenate(blocks, axis=dim)
 
 
 def joined(part, axis, combine):
@@ -41,7 +46,7 @@
     ctx_pages = page_table.shape[1]
     col_count = queries.shape[1]
     highest = lax.Precision.HIGHEST
-    all_queries = lax.all_gather(queries, "seq", axis=1, tiled=True)
+    all_queries = gather_blocks(queries, "seq", 1)
     head_count = all_queries.shape[1] // HEAD_DIM
     group_size = head_count // kv_heads
     score_scale = 1.0 / math.sqrt(HEAD_DIM)

time: 193 us -> 193 us (level)
  no operation moved by 1% of the time
where the time goes in v1:
time: 193 us; the launch traced here: 191 us
  blocking collectives  97.4 us (50%)
  local copies, waits for them, and re-layouts  41.4 us (21%)
  other arithmetic  23.8 us (12%)
  matrix products  14.6 us (8%)
  between operations  13.6 us (7%)
    all_gather x4, blocking collectives, joined(): gathered = jax.tree.map(lambda a: lax.all_gather(a, axis), part)  74 us
    all_gather x1, blocking collectives, gather_blocks(): blocks = lax.all_gather(block, mesh_axis)  23.4 us
    add x15, other arithmetic, merge_pair(): left[offset + 2] * left_scale[..., None]  16.9 us
    dynamic_slice x21, local copies, waits for them, and re-layouts, take(): lax.dynamic_index_in_dim(a, source, 0, False)  14.4 us
    unnamed x11, local copies, waits for them, and re-layouts  13 us
    slice x1, local copies, waits for them, and re-layouts, per_device(): kv_pool[:, :, kv_width:].reshape(slot_count, page_len, kv_heads, HEAD_DIM)  6.11 us
    dot_general x1, matrix products, per_device(): jnp.einsum('skgt,stkd->skgd', page_wt, value_rows, preferred_element_type...  4.5 us
  transfers between devices with their start and end apart: 2, of which 0 were waited for; matrix products, arithmetic and copies ran while one was open for 7% of the time, Pallas kernels for 0%

profile of v1, /device:TPU:0, one launch (start us, length us, event | category | flops | bytes accessed | tf_op | source)
XLA Modules:
  0.0 191.3 jit_solution(13230901904686127513)
XLA Ops:
  9.3 23.4 %all-gather.7 = bf16[16,4,256]{2,1,0:T(4,128)(2,1)S(1)} all-gather(bf16[1,4,256]{2,1,0:T(4,128)(2,1)} %bitcast.111), channel_id=2, replica_groups=mesh['grp'=2,'seq'=16] {'seq'}, dimensions={0}, use_global_device_ids=true | all-gather | bytes 34816 | tf_op jit(solution)/shard_map/all_gather | solution.py:12
  33.1 6.1 %fusion.43 = (bf16[16,128,1024]{2,1,0:T(8,128)(2,1)}, bf16[16,128,1024]{2,1,0:T(8,128)(2,1)}) fusion(bf16[16,128,2048]{2,1,0:T(8,128)(2,1)} %param.10), kind=kLoop, calls=%fused_computation.82 | loop fusion | bytes 16777216 | tf_op jit(solution)/shard_map/slice | solution.py:65
  39.2 6.4 %copy.115 = bf16[16,128,1024]{1,2,0:T(8,128)(2,1)} copy(bf16[16,128,1024]{2,1,0:T(8,128)(2,1)} %get-tuple-element.421) | data formatting | bytes 8388608
  45.6 6.4 %copy.114 = bf16[16,128,1024]{1,2,0:T(8,128)(2,1)} copy(bf16[16,128,1024]{2,1,0:T(8,128)(2,1)} %get-tuple-element.422) | data formatting | bytes 8388608
  52.0 3.5 %fusion.31 = f32[16,1,8,128]{3,1,2,0:T(1,128)S(1)} fusion(bf16[16,128,8,128]{1,3,2,0:T(8,128)(2,1)} %bitcast.96, pred[16,128,1,1]{1,0,2,3:T(8,128)(4,1)S(1)} %get-tuple-element.428), kind=kOutput, calls=%fused_computation.61 | convolution fusion | flops 4194304 | bytes 4261888 | tf_op jit(solution)/shard_map/st,stkd->skd/dot_general | solution.py:76
  55.5 1.2 fusion.33
  58.5 1.2 compare_reduce_fusion
  59.9 3.5 %fusion.45 = (f32[16,8,4]{2,1,0:T(8,128)S(1)}, f32[16,8,4,128]{3,2,1,0:T(4,128)S(1)}) fusion(bf16[16,8,4,128]{3,2,1,0:T(4,128)(2,1)S(1)} %reshape.113, bf16[16,128,8,128]{1,3,2,0:T(8,128)(2,1)} %bitcast.98, pred[16,128]{1,0:T(8,128)(4,1)S(1)} %get-tuple-element.427), kind=kOutput, calls=%fused_computation.84 | convolution fusion | flops 16973312 | bytes 4591616 | tf_op jit(solution)/shard_map/skgd,stkd->skgt/dot_general | solution.py:92
  63.7 4.5 %fusion.40 = f32[16,8,4,128]{3,2,1,0:T(4,128)S(1)} fusion(bf16[16,128,8,128]{1,3,2,0:T(8,128)(2,1)} %bitcast.97, f32[16,8,4,128]{3,2,1,0:T(4,128)S(1)} %get-tuple-element.430, f32[16,8,4]{2,1,0:T(8,128)S(1)} %get-tuple-element.429, pred[16,128]{1,0:T(8,128)(4,1)S(1)} %get-tuple-element.427), kind=kOutput, calls=%fused_computation.81 | convolution fusion | flops 16973824 | bytes 4722688 | tf_op jit(solution)/shard_map/skgt,stkd->skgd/dot_general | solution.py:102
  70.9 18.0 %all-gather.2 = f32[64,8,4]{1,2,0:T(4,128)S(1)} all-gather(f32[4,8,4]{1,2,0:T(4,128)S(1)} %copy.87), channel_id=4, replica_groups=mesh['grp'=2,'seq'=16] {'seq'}, dimensions={0}, use_global_device_ids=true | all-gather | bytes 8704 | tf_op jit(solution)/shard_map/all_gather | solution.py:17
  88.9 19.0 %all-gather.1 = f32[64,8,4]{1,2,0:T(4,128)S(1)} all-gather(f32[4,8,4]{1,2,0:T(4,128)S(1)} %copy.86), channel_id=3, replica_groups=mesh['grp'=2,'seq'=16] {'seq'}, dimensions={0}, use_global_device_ids=true | all-gather | bytes 8704 | tf_op jit(solution)/shard_map/all_gather | solution.py:17
  107.9 18.0 %all-gather.5 = f32[64,8,4]{1,2,0:T(4,128)S(1)} all-gather(f32[4,8,4]{1,2,0:T(4,128)S(1)} %copy.95), channel_id=7, replica_groups=mesh['grp'=2,'seq'=16] {'seq'}, dimensions={0}, use_global_device_ids=true | all-gather | bytes 8704 | tf_op jit(solution)/shard_map/all_gather | solution.py:17
  125.9 19.0 %all-gather.4 = f32[64,8,4]{1,2,0:T(4,128)S(1)} all-gather(f32[4,8,4]{1,2,0:T(4,128)S(1)} %copy.93), channel_id=6, replica_groups=mesh['grp'=2,'seq'=16] {'seq'}, dimensions={0}, use_global_device_ids=true | all-gather | bytes 8704 | tf_op jit(solution)/shard_map/all_gather | solution.py:17
  146.7 36.7 %while.25 = (s32[]{:T(128)}, f32[4,8,4]{1,2,0:T(4,128)S(1)}, f32[4,8,4]{1,2,0:T(4,128)S(1)}, f32[4,8,4,128]{3,2,1,0:T(4,128)S(1)}, f32[4,8,4]{1,2,0:T(4,128)S(1)...) while((s32[]{:T(128)}, f32[4,8,4]{1,2,0:T(4,128)S(1)}, ...), condition=%wide.region_12.13_spmd, body=%wide.region_11.12_spmd.sunk | while | flops 99845 | bytes 538823 | solution.py:22
  148.0 1.1 fusion.60
  150.4 1.1 fusion.60
  152.9 1.1 fusion.60
  155.3 1.1 fusion.60
  157.8 1.1 fusion.60
  160.2 1.1 fusion.60
  162.7 1.1 fusion.60
  170.0 1.1 fusion.60
  174.9 1.1 fusion.60
  179.8 1.1 fusion.60
  (174 shorter events, 35.8 us)
Async XLA Ops:
  6.5 138.4 %all-gather.11.cloned.1.call-start = ((), (), s32[]{:S(2)}) async-start(), calls=%async_computation | async-start | bytes 1114112 | tf_op jit(solution)/shard_map/all_gather | solution.py:17
  52.0 3.5 %copy-start = (bf16[16,128,1024]{1,2,0:T(8,128)(2,1)S(1)}, bf16[16,128,1024]{1,2,0:T(8,128)(2,1)}, u32[]{:S(2)}) copy-start(bf16[16,128,1024]{1,2,0:T(8,128)(2,1)} %copy.114) | copy-start | bytes 12582916
  52.0 6.5 %copy-start.1 = (s32[4,8,16]{2,1,0:T(8,128)S(1)}, s32[4,8,16]{2,1,0:T(8,128)}, u32[]{:S(2)}) copy-start(s32[4,8,16]{2,1,0:T(8,128)} %param.12) | copy-start | bytes 6148
  58.5 87.3 %all-gather.13.cloned.1.call-start = ((), (), s32[]{:S(2)}) async-start(), calls=%async_computation.1 | async-start | bytes 1114112 | tf_op jit(solution)/shard_map/all_gather | solution.py:17
  59.9 9.7 %copy-start.2 = (f32[4,64]{1,0:T(4,128)S(1)}, f32[4,64]{1,0:T(4,128)}, u32[]{:S(2)}) copy-start(f32[4,64]{1,0:T(4,128)} %param.9) | copy-start | bytes 3076
Sparse Core Ops, SparseCore 0:
  58.6 34.1 all-gather.10
  94.9 37.5 all-gather.12
